TPU v7x, 256 devices: a whole 4x4x8 slice. The times are simulated.
256 devices in a mesh: dp: 8 (over y, core), tensor: 32 (over z, x).
Axes of the slice: x: 4, y: 4, z: 8, core: 2. Of those that a mesh axis runs over, the one named last changes fastest.
Arguments:
- hidden: bfloat16 [1280, 16384], P(None, ('dp', 'tensor')), may hold values from -100 to 100
- gain: bfloat16 [1, 16384], P(None, ('dp', 'tensor')), may hold values from 0.5 to 2, as said below
- head_weight: bfloat16 [16384, 65536], P('dp', 'tensor'), may hold values from -3 to 3
- draft_probs: float32 [1280, 65536], P(('dp', 'tensor')), may hold values from 0 to 1, as said below
- draft_ids: int32 [1280], P('dp'), may hold values from 0 to 65535
- reject_at: int32 [256], P('dp'), may hold values from 0 to 4
Outputs:
- token_logprob: float32 [1280], P('dp')
- residual: float32 [256, 65536], P('dp', 'tensor')
Inputs may be any that keep to these rules, and one draw needn't show every extreme that they name: `draft_probs`: every row is a probability distribution over the 65536 entries that sums to one. `gain`: positive.
All inputs are finite; a program needn't handle non-finite values.
Results may differ from a plain program's by a relative error of at most 0.0005.
The roundings to bfloat16 on the way count: a program that leaves them out, or rounds other values in their place, can miss the bound.
Values may be sent and summed in bfloat16 or wider, within the bound.
A program may use at most 128 MiB of HBM per device.

v0:
```python
import jax
import jax.numpy as jnp
from jax import lax
from jax.sharding import Mesh
from jax.sharding import PartitionSpec as P

D = 16384
VOCAB = 65536
POS = 5
TENSOR = ("tensor_0", "tensor_1")
DP_TENSOR = ("dp", "tensor_0", "tensor_1")
EPS = 1e-05


def gather_turned(arrays, axis, dims):
    turned = [jnp.moveaxis(a, dim, 0) for a, dim in zip(arrays, dims)]
    widths = [t[0].size for t in turned]
    both = jnp.concatenate([t.reshape(-1, w) for t, w in zip(turned, widths)], axis=1)
    out = lax.all_gather(both, axis, axis=0, tiled=True)
    tiles = jnp.split(out, [sum(widths[:k]) for k in range(1, len(widths))], axis=1)
    return tuple(
        (
            jnp.moveaxis(b.reshape(-1, *t.shape[1:]), 0, dim)
            for b, t, dim in zip(tiles, turned, dims)
        )
    )


def sent_to_all(shard, axis):
    devices = lax.axis_size(axis)
    return lax.all_to_all(
        jnp.broadcast_to(shard[None], (devices, *shard.shape)), axis, 0, 0, tiled=True
    )


def of_everyone(shard, axis):
    everything = sent_to_all(shard, axis)
    return jnp.sum(everything, axis=0)


def collected_together(shard, axis):
    leaves = jax.tree.leaves(shard)
    order = sorted(range(len(leaves)), key=lambda k: -leaves[k].size)
    width = (1, *leaves[order[0]].shape)[-1]
    lines = [
        jnp.pad(leaves[k].reshape(-1), (0, -leaves[k].size % width)).reshape(-1, width)
        for k in order
    ]
    both, at, found = (sent_to_all(jnp.concatenate(lines), axis), 0, {})
    for k, line in zip(order, lines):
        share = both[:, at : at + len(line)].reshape(len(both), -1)
        found[k] = share[:, : leaves[k].size].reshape(-1, *leaves[k].shape)
        at += len(line)
    numbers = iter(range(len(leaves)))
    return jax.tree.map(lambda _: found[next(numbers)], shard)


def combined_pairwise(pieces, combine):
    while len(jax.tree.leaves(pieces)[0]) > 1:
        pieces = jax.vmap(combine)(
            *(jax.tree.map(lambda part: part[side::2], pieces) for side in (0, 1))
        )
    return jax.tree.map(lambda part: part[0], pieces)


def merged(shard, axis, combine):
    pieces = collected_together(shard, axis)
    return combined_pairwise(pieces, combine)


def in_blocks(shard, dim, devices):
    before, after = (shard.shape[:dim], shard.shape[dim + 1 :])
    return jnp.moveaxis(shard.reshape(*before, devices, -1, *after), dim, 0)


def laid_out(tiles, dim):
    tiles = jnp.moveaxis(tiles, 0, dim)
    shape = tiles.shape
    return tiles.reshape(*shape[:dim], shape[dim] * shape[dim + 1], *shape[dim + 2 :])


def exchange_in_order(tiles, axes, order):
    inside = tiles.shape[1:]
    out = tiles.reshape(*(lax.axis_size(a) for a in axes), *inside)
    for k in order:
        out = lax.all_to_all(out, axes[k], k, k, tiled=True)
    return out.reshape(-1, *inside)


def stepwise_exchange(shard, axes, order, split_dim, concat_dim):
    tiles = in_blocks(shard, split_dim, lax.axis_size(axes))
    return laid_out(exchange_in_order(tiles, axes, order), concat_dim)


def combine_stats(first, second):
    top = jnp.maximum(first[0], second[0])
    total = first[1] * jnp.exp(first[0] - top) + second[1] * jnp.exp(second[0] - top)
    return (top, total, first[2] + second[2])


def shards(hidden, gain, head_weight, draft_probs, draft_ids, reject_at):
    raw, gains = gather_turned((hidden, gain), TENSOR, (1, 1))
    values = raw.astype(jnp.float32)
    squares = of_everyone(jnp.sum(values * values, axis=1), "dp")
    normed = (values * lax.rsqrt(squares / D + EPS)[:, None] * gains.astype(jnp.float32)).astype(
        jnp.bfloat16
    )
    logits = lax.psum_scatter(
        jnp.dot(normed, head_weight, preferred_element_type=jnp.float32),
        "dp",
        scatter_dimension=0,
        tiled=True,
    )
    width = logits.shape[1]
    columns = lax.broadcasted_iota(jnp.int32, (1, width), 1) + lax.axis_index(TENSOR) * width
    local_max = jnp.max(logits, axis=1)
    local_pick = jnp.sum(jnp.where(columns == draft_ids[:, None], logits, 0.0), axis=1)
    local_total = jnp.sum(jnp.exp(logits - local_max[:, None]), axis=1)
    top, total, picked = merged((local_max, local_total, local_pick), TENSOR, combine_stats)
    logz = top + jnp.log(total)
    token_logprob = picked - logz
    requests = reject_at.shape[0]
    where_at = reject_at[:, None, None]
    chosen = jnp.take_along_axis(logits.reshape(requests, POS, width), where_at, axis=1)[:, 0]
    chosen_logz = jnp.take_along_axis(logz.reshape(requests, POS), reject_at[:, None], axis=1)[:, 0]
    owned = draft_probs.shape[0] // POS
    mine = lax.dynamic_slice_in_dim(reject_at, lax.axis_index(TENSOR) * owned, owned, 0)
    local_rows = jnp.take_along_axis(
        draft_probs.reshape(owned, POS, draft_probs.shape[1]), mine[:, None, None], axis=1
    )[:, 0]
    drafts = stepwise_exchange(local_rows, TENSOR, (0, 1), 1, 0)
    target = jnp.exp(chosen - chosen_logz[:, None])
    kept = jnp.maximum(target - drafts, 0.0)
    mass = of_everyone(jnp.sum(kept, axis=1), TENSOR)
    residual = VOCAB * kept / mass[:, None]
    return (token_logprob, residual)


def solution(mesh):
    finer = Mesh(mesh.devices.reshape(mesh.shape["dp"], 8, 4), ("dp", "tensor_0", "tensor_1"))
    return jax.shard_map(
        shards,
        mesh=finer,
        in_specs=(
            P(None, DP_TENSOR),
            P(None, DP_TENSOR),
            P("dp", TENSOR),
            P(DP_TENSOR, None),
            P("dp"),
            P("dp"),
        ),
        out_specs=(P("dp"), P("dp", TENSOR)),
        check_vma=False,
    )
```

profile of v0, /device:TPU:2, one launch (start us, length us, event | category | flops | bytes accessed | tf_op | source)
XLA Modules:
  0.0 244.7 jit_solution(11810999547633045622)
XLA Ops:
  7.2 0.0 all-gather.2.cloned.1.call-start
  7.2 0.8 copy.43
  8.0 1.6 pad_maximum_fusion
  9.6 0.0 all-gather.2.cloned.1.call-update
  9.6 89.8 %all-gather.2.cloned.1.call-done = bf16[2048,1281]{1,0:T(8,128)(2,1)} async-done(((bf16[64,1281]{1,0:T(8,128)(2,1)}), bf16[2048,1281]{1,0:T(8,128)(2,1)}) %all-gather.2.cloned.1.call-update) | async-done | bytes 5246992 | tf_op jit(solution)/shard_map/all_gather | solution.py:19
  99.4 3.6 %fusion = f32[1280]{0:T(1024)S(1)} fusion(bf16[2048,1281]{1,0:T(8,128)(2,1)} %all-gather.2.cloned.1.call-done), kind=kLoop, calls=%fused_computation.4 | loop fusion | flops 7863040 | bytes 5248000 | tf_op jit(solution)/shard_map/reduce_sum | solution.py:104
  103.0 0.6 broadcast_in_dim.59
  103.6 4.3 %all-to-all-start = ((f32[8,1,1280]{2,1,0:T(1,128)}), f32[8,1,1280]{2,1,0:T(1,128)S(1)}, u32[]{:S(2)}, u32[]{:S(2)}) async-start(f32[8,1,1280]{2,1,0:T(1,128)} %broadcast_in_dim.59), calls=%async_computation | async-start | bytes 81920 | tf_op jit(solution)/shard_map/all_to_all | solution.py:31
  107.9 0.0 reduce-scatter.2.cloned.1.call-start
  108.0 1.3 convert_reduce_fusion
  109.2 4.2 %all-to-all-done = f32[8,1,1280]{2,1,0:T(1,128)S(1)} async-done(((f32[8,1,1280]{2,1,0:T(1,128)}), f32[8,1,1280]{2,1,0:T(1,128)S(1)}, u32[]{:S(2)}, u32[]{:S(2)}) %all-to-all-start) | async-done | bytes 40992 | tf_op jit(solution)/shard_map/all_to_all | solution.py:31
  113.5 17.9 %fusion.3 = f32[1280,2048]{1,0:T(8,128)} fusion(bf16[2048,2048]{1,0:T(8,128)(2,1)} %param.8, f32[2048]{0:T(1024)S(1)} %convert_reduce_fusion, f32[1280]{0:T(1024)S(1)} %add_rsqrt_fusion, bf16[2048,1281]{1,0:T(8,128)(2,1)} %all-gather.2.cloned.1.call-done), kind=kOutput, calls=%fused_computation.7 | convolution fusion | flops 10747904000 | bytes 24130560 | tf_op jit(solution)/shard_map/dot_general | solution.py:109
  131.3 0.0 copy-start.2
  131.3 0.0 copy-start.1
  131.3 0.0 reduce-scatter.2.cloned.1.call-update
  131.4 0.6 copy-done.2
  132.0 0.6 dynamic_slice.3
  134.5 2.4 fusion.8
  136.9 0.8 select_n.68
  137.7 4.0 %all-to-all-start.2 = ((f32[8,4,1,2048]{3,1,2,0:T(4,128)}), f32[8,4,1,2048]{3,1,2,0:T(4,128)S(1)}, u32[]{:S(2)}, u32[]{:S(2)}) async-start(f32[8,4,1,2048]{3,1,2,0:T(4,128)} %select_n.68), calls=%async_computation.3 | async-start | bytes 524288 | tf_op jit(solution)/shard_map/all_to_all | solution.py:86
  141.8 11.8 %all-to-all-done.2 = f32[8,4,1,2048]{3,1,2,0:T(4,128)S(1)} async-done(((f32[8,4,1,2048]{3,1,2,0:T(4,128)}), f32[8,4,1,2048]{3,1,2,0:T(4,128)S(1)}, u32[]{:S(2)}, u32[]{:S(2)}) %all-to-all-start.2) | async-done | bytes 262176 | tf_op jit(solution)/shard_map/all_to_all | solution.py:86
  153.5 0.9 copy.48
  154.4 5.2 %all-to-all-start.3 = ((f32[8,4,1,2048]{3,0,2,1:T(8,128)}), f32[8,4,1,2048]{3,0,2,1:T(8,128)S(1)}, u32[]{:S(2)}, u32[]{:S(2)}) async-start(f32[8,4,1,2048]{3,0,2,1:T(8,128)} %copy.48), calls=%async_computation.4 | async-start | bytes 524288 | tf_op jit(solution)/shard_map/all_to_all | solution.py:86
  159.6 33.1 %reduce-scatter.2.cloned.1.call-done = f32[160,2048]{1,0:T(8,128)} async-done(((f32[1280,2048]{1,0:T(8,128)}), f32[160,2048]{1,0:T(8,128)}) %reduce-scatter.2.cloned.1.call-update) | async-done | bytes 1310736 | tf_op jit(solution)/shard_map/reduce_scatter | solution.py:108
  192.7 1.5 reduce_max.9
  194.1 0.0 copy-done.1
  194.1 1.8 exponential_reduce_fusion
  196.0 0.8 reshape.248
  196.8 0.0 all-to-all-done.3
  196.8 0.0 copy-start
  196.8 10.2 %all-to-all-start.1 = ((f32[32,1,480]{2,1,0:T(1,128)}), f32[32,1,480]{2,1,0:T(1,128)S(1)}, u32[]{:S(2)}, u32[]{:S(2)}) async-start(f32[32,1,480]{2,1,0:T(1,128)} %reshape.248), calls=%async_computation.2 | async-start | bytes 131072 | tf_op jit(solution)/shard_map/all_to_all | solution.py:31
  207.0 0.2 copy.49
  207.1 0.0 copy-done
  207.2 0.8 reshape_reshape.3
  208.0 1.5 reshape.176
  209.4 0.8 copy.47
  210.2 0.9 gather_fusion
  211.1 0.1 gather.23
  211.1 4.5 %all-to-all-done.1 = f32[32,1,480]{2,1,0:T(1,128)S(1)} async-done(((f32[32,1,480]{2,1,0:T(1,128)}), f32[32,1,480]{2,1,0:T(1,128)S(1)}, u32[]{:S(2)}, u32[]{:S(2)}) %all-to-all-start.1) | async-done | bytes 61472 | tf_op jit(solution)/shard_map/all_to_all | solution.py:31
  215.6 0.5 broadcast.165
  216.2 0.8 reduce.15
  217.0 0.1 reshape.249
  217.1 0.1 fusion.19
  217.8 0.5 broadcast.164
  218.3 0.7 fusion.18
  219.0 0.1 add.104
  219.1 0.7 gather_fusion.1
  219.8 0.1 sub.88
  219.9 0.1 copy.52
  220.0 0.1 broadcast_in_dim.68
  220.1 0.1 copy.50
  220.2 1.2 fusion.13
  221.4 0.1 copy.53
  221.5 0.1 broadcast_in_dim.71
  221.6 0.6 broadcast_in_dim.72
  222.2 5.3 %all-to-all-start.4 = ((f32[32,1,32]{2,1,0:T(1,128)}), f32[32,1,32]{2,1,0:T(1,128)S(1)}, u32[]{:S(2)}, u32[]{:S(2)}) async-start(f32[32,1,32]{2,1,0:T(1,128)} %broadcast_in_dim.72), calls=%async_computation.5 | async-start | bytes 32768 | tf_op jit(solution)/shard_map/all_to_all | solution.py:31
  227.5 0.6 fusion.15
  228.1 8.0 %all-to-all-done.4 = f32[32,1,32]{2,1,0:T(1,128)S(1)} async-done(((f32[32,1,32]{2,1,0:T(1,128)}), f32[32,1,32]{2,1,0:T(1,128)S(1)}, u32[]{:S(2)}, u32[]{:S(2)}) %all-to-all-start.4) | async-done | bytes 4128 | tf_op jit(solution)/shard_map/all_to_all | solution.py:31
  236.1 1.8 multiply_divide_fusion
  (45 shorter events, 0.7 us)
Async XLA Ops:
  7.2 92.2 %all-gather.2.cloned.1.call-start = ((), (), s32[]{:S(2)}) async-start(), calls=%async_computation.6 | async-start | bytes 5947392 | tf_op jit(solution)/shard_map/all_gather | solution.py:19
  103.6 9.8 %all-to-all-start = ((f32[8,1,1280]{2,1,0:T(1,128)}), f32[8,1,1280]{2,1,0:T(1,128)S(1)}, u32[]{:S(2)}, u32[]{:S(2)}) async-start(f32[8,1,1280]{2,1,0:T(1,128)} %broadcast_in_dim.59), calls=%async_computation | async-start | bytes 81920 | tf_op jit(solution)/shard_map/all_to_all | solution.py:31
  107.9 84.8 %reduce-scatter.2.cloned.1.call-start = ((), (), s32[]{:S(2)}) async-start(), calls=%async_computation.7 | async-start | bytes 11796480 | tf_op jit(solution)/shard_map/reduce_scatter | solution.py:108
  131.3 0.7 copy-start.2
  131.3 62.8 %copy-start.1 = (s32[160]{0:T(256)S(1)}, s32[160]{0:T(256)}, u32[]{:S(2)}) copy-start(s32[160]{0:T(256)} %param.10) | copy-start | bytes 1924
  137.7 15.8 %all-to-all-start.2 = ((f32[8,4,1,2048]{3,1,2,0:T(4,128)}), f32[8,4,1,2048]{3,1,2,0:T(4,128)S(1)}, u32[]{:S(2)}, u32[]{:S(2)}) async-start(f32[8,4,1,2048]{3,1,2,0:T(4,128)} %select_n.68), calls=%async_computation.3 | async-start | bytes 524288 | tf_op jit(solution)/shard_map/all_to_all | solution.py:86
  154.4 42.4 %all-to-all-start.3 = ((f32[8,4,1,2048]{3,0,2,1:T(8,128)}), f32[8,4,1,2048]{3,0,2,1:T(8,128)S(1)}, u32[]{:S(2)}, u32[]{:S(2)}) async-start(f32[8,4,1,2048]{3,0,2,1:T(8,128)} %copy.48), calls=%async_computation.4 | async-start | bytes 524288 | tf_op jit(solution)/shard_map/all_to_all | solution.py:86
  196.8 10.4 %copy-start = (f32[8,4,1,2048]{3,0,2,1:T(8,128)}, f32[8,4,1,2048]{3,0,2,1:T(8,128)S(1)}, u32[]{:S(2)}) copy-start(f32[8,4,1,2048]{3,0,2,1:T(8,128)S(1)} %all-to-all-done.3) | copy-start | bytes 786436
  196.8 18.8 %all-to-all-start.1 = ((f32[32,1,480]{2,1,0:T(1,128)}), f32[32,1,480]{2,1,0:T(1,128)S(1)}, u32[]{:S(2)}, u32[]{:S(2)}) async-start(f32[32,1,480]{2,1,0:T(1,128)} %reshape.248), calls=%async_computation.2 | async-start | bytes 131072 | tf_op jit(solution)/shard_map/all_to_all | solution.py:31
  222.2 13.8 %all-to-all-start.4 = ((f32[32,1,32]{2,1,0:T(1,128)}), f32[32,1,32]{2,1,0:T(1,128)S(1)}, u32[]{:S(2)}, u32[]{:S(2)}) async-start(f32[32,1,32]{2,1,0:T(1,128)} %broadcast_in_dim.72), calls=%async_computation.5 | async-start | bytes 32768 | tf_op jit(solution)/shard_map/all_to_all | solution.py:31
Sparse Core Ops, SparseCore 0:
  11.1 88.2 all-gather.1
  131.5 61.1 reduce-scatter.1
where the time goes:
time: 245 us
  waiting for transfers between devices  151 us (62%)
  starting transfers between devices  29 us (12%)
  matrix products  17.9 us (7%)
  other arithmetic  17.3 us (7%)
  between operations  16.2 us (7%)
  local copies, waits for them, and re-layouts  12.9 us (5%)
    all_gather x1, waiting for transfers between devices, gather_turned(): out = lax.all_gather(both, axis, axis=0, tiled=True)  89.8 us
    reduce_scatter x1, waiting for transfers between devices, shards(): lax.psum_scatter(jnp.dot(normed, head_weight, preferred_element_type=jnp....  33.1 us
    all_to_all x3, starting transfers between devices, sent_to_all(): lax.all_to_all(jnp.broadcast_to(shard[None], (devices, *shard.shape)), ax...  19.7 us
    dot_general x1, matrix products, shards(): jnp.dot(normed, head_weight, preferred_element_type=jnp.float32)  17.9 us
    all_to_all x3, waiting for transfers between devices, sent_to_all(): lax.all_to_all(jnp.broadcast_to(shard[None], (devices, *shard.shape)), ax...  16.7 us
    all_to_all x2, waiting for transfers between devices, exchange_in_order(): out = lax.all_to_all(out, axes[k], k, k, tiled=True)  11.8 us
    all_to_all x2, starting transfers between devices, exchange_in_order(): out = lax.all_to_all(out, axes[k], k, k, tiled=True)  9.18 us
  transfers between devices with their start and end apart: 7, of which 6 were waited for; matrix products, arithmetic and copies ran while one was open for 6% of the time, Pallas kernels for 0%

commit v1 on v0

--- a/solution.py
+++ b/solution.py
@@ -16,7 +16,9 @@
     turned = [jnp.moveaxis(a, dim, 0) for a, dim in zip(arrays, dims)]
     widths = [t[0].size for t in turned]
     both = jnp.concatenate([t.reshape(-1, w) for t, w in zip(turned, widths)], axis=1)
-    out = lax.all_gather(both, axis, axis=0, tiled=True)
+    out = jnp.concatenate(
+        lax.all_to_all(jnp.stack([both] * lax.axis_size(axis)), axis, 0, 0), axis=0
+    )
     tiles = jnp.split(out, [sum(widths[:k]) for k in range(1, len(widths))], axis=1)
     return tuple(
         (

time: 245 us -> 295 us (1.20)
  blocking collectives: 0 us -> 141 us
  waiting for transfers between devices: 151 us -> 61.2 us
  local copies, waits for them, and re-layouts: 12.9 us -> 16.1 us
  other arithmetic: 17.3 us -> 14.2 us
    all_to_all x0 -> x1, blocking collectives: none -> 141 us  [gather_turned(): lax.all_to_all(jnp.stack([both] * lax.axis_size(axis)), axis, 0, 0)]
    all_gather x1 -> x0, waiting for transfers between devices: 89.8 us -> none  [gather_turned(): out = lax.all_gather(both, axis, axis=0, tiled=True)]
  transfers between devices with their start and end apart: 7 -> 6, of which waited for: 6 -> 5; matrix products, arithmetic and copies ran while one was open for 6% -> 5% of each run, Pallas kernels for 0% -> 0%
where the time goes in v1:
time: 295 us; the launch traced here: 294 us
  blocking collectives  141 us (48%)
  waiting for transfers between devices  61.2 us (21%)
  starting transfers between devices  28.2 us (10%)
  matrix products  17.9 us (6%)
  between operations  16.2 us (5%)
  local copies, waits for them, and re-layouts  16.1 us (5%)
  other arithmetic  14.2 us (5%)
    all_to_all x1, blocking collectives, gather_turned(): lax.all_to_all(jnp.stack([both] * lax.axis_size(axis)), axis, 0, 0)  141 us
    reduce_scatter x1, waiting for transfers between devices, shards(): lax.psum_scatter(jnp.dot(normed, head_weight, preferred_element_type=jnp....  32.6 us
    all_to_all x3, starting transfers between devices, sent_to_all(): lax.all_to_all(jnp.broadcast_to(shard[None], (devices, *shard.shape)), ax...  19.9 us
    dot_general x1, matrix products, shards(): jnp.dot(normed, head_weight, preferred_element_type=jnp.float32)  17.9 us
    all_to_all x3, waiting for transfers between devices, sent_to_all(): lax.all_to_all(jnp.broadcast_to(shard[None], (devices, *shard.shape)), ax...  16.7 us
    all_to_all x2, waiting for transfers between devices, exchange_in_order(): out = lax.all_to_all(out, axes[k], k, k, tiled=True)  12 us
    all_to_all x2, starting transfers between devices, exchange_in_order(): out = lax.all_to_all(out, axes[k], k, k, tiled=True)  8.21 us
  transfers between devices with their start and end apart: 6, of which 5 were waited for; matrix products, arithmetic and copies ran while one was open for 5% of the time, Pallas kernels for 0%

profile of v1, /device:TPU:2, one launch (start us, length us, event | category | flops | bytes accessed | tf_op | source)
XLA Modules:
  0.0 294.4 jit_solution(1211645814927416341)
XLA Ops:
  7.2 0.8 copy.46
  7.9 0.9 pad_maximum_fusion
  8.9 0.7 stack.2
  9.6 140.6 %all_to_all.32 = bf16[32,64,1281]{2,1,0:T(8,128)(2,1)S(1)} all-to-all(bf16[32,64,1281]{2,1,0:T(8,128)(2,1)S(1)} %stack.2), channel_id=1, replica_groups=mesh['dp'=8,'tensor_0'=8,'tensor_1'=4] {'tensor_0','tensor_1'}, dimensions={0} | all-to-all | bytes 10493952 | tf_op jit(solution)/shard_map/all_to_all | solution.py:20
  150.2 0.0 copy-start
  150.2 2.5 copy-done
  152.6 1.1 fusion
  153.7 0.6 broadcast_in_dim.59
  154.4 4.5 %all-to-all-start.1 = ((f32[8,1,1280]{2,1,0:T(1,128)}), f32[8,1,1280]{2,1,0:T(1,128)S(1)}, u32[]{:S(2)}, u32[]{:S(2)}) async-start(f32[8,1,1280]{2,1,0:T(1,128)} %broadcast_in_dim.59), calls=%async_computation.1 | async-start | bytes 81920 | tf_op jit(solution)/shard_map/all_to_all | solution.py:33
  158.9 0.0 reduce-scatter.2.cloned.1.call-start
  158.9 1.3 convert_reduce_fusion
  160.2 4.2 %all-to-all-done.1 = f32[8,1,1280]{2,1,0:T(1,128)S(1)} async-done(((f32[8,1,1280]{2,1,0:T(1,128)}), f32[8,1,1280]{2,1,0:T(1,128)S(1)}, u32[]{:S(2)}, u32[]{:S(2)}) %all-to-all-start.1) | async-done | bytes 40992 | tf_op jit(solution)/shard_map/all_to_all | solution.py:33
  164.4 17.9 %fusion.3 = f32[1280,2048]{1,0:T(8,128)} fusion(bf16[2048,2048]{1,0:T(8,128)(2,1)} %param.8, f32[2048]{0:T(1024)S(1)} %convert_reduce_fusion, f32[1280]{0:T(1024)S(1)} %add_rsqrt_fusion, bf16[2048,1281]{1,0:T(8,128)(2,1)} %bitcast.29), kind=kOutput, calls=%fused_computation.7 | convolution fusion | flops 10747904000 | bytes 24130560 | tf_op jit(solution)/shard_map/dot_general | solution.py:111
  182.3 0.0 copy-start.3
  182.3 0.0 copy-start.2
  182.3 0.0 reduce-scatter.2.cloned.1.call-update
  182.3 0.6 copy-done.3
  182.9 0.6 dynamic_slice.3
  185.5 2.4 fusion.8
  187.9 0.8 select_n.68
  188.7 3.4 %all-to-all-start.3 = ((f32[8,4,1,2048]{3,1,2,0:T(4,128)}), f32[8,4,1,2048]{3,1,2,0:T(4,128)S(1)}, u32[]{:S(2)}, u32[]{:S(2)}) async-start(f32[8,4,1,2048]{3,1,2,0:T(4,128)} %select_n.68), calls=%async_computation.4 | async-start | bytes 524288 | tf_op jit(solution)/shard_map/all_to_all | solution.py:88
  192.1 12.0 %all-to-all-done.3 = f32[8,4,1,2048]{3,1,2,0:T(4,128)S(1)} async-done(((f32[8,4,1,2048]{3,1,2,0:T(4,128)}), f32[8,4,1,2048]{3,1,2,0:T(4,128)S(1)}, u32[]{:S(2)}, u32[]{:S(2)}) %all-to-all-start.3) | async-done | bytes 262176 | tf_op jit(solution)/shard_map/all_to_all | solution.py:88
  204.1 0.9 copy.51
  205.0 4.8 %all-to-all-start.4 = ((f32[8,4,1,2048]{3,0,2,1:T(8,128)}), f32[8,4,1,2048]{3,0,2,1:T(8,128)S(1)}, u32[]{:S(2)}, u32[]{:S(2)}) async-start(f32[8,4,1,2048]{3,0,2,1:T(8,128)} %copy.51), calls=%async_computation.5 | async-start | bytes 524288 | tf_op jit(solution)/shard_map/all_to_all | solution.py:88
  209.8 32.6 %reduce-scatter.2.cloned.1.call-done = f32[160,2048]{1,0:T(8,128)} async-done(((f32[1280,2048]{1,0:T(8,128)}), f32[160,2048]{1,0:T(8,128)}) %reduce-scatter.2.cloned.1.call-update) | async-done | bytes 1310736 | tf_op jit(solution)/shard_map/reduce_scatter | solution.py:110
  242.3 1.5 reduce_max.9
  243.8 0.0 copy-done.2
  243.8 1.8 exponential_reduce_fusion
  245.6 0.8 reshape.254
  246.4 0.0 all-to-all-done.4
  246.5 0.0 copy-start.1
  246.5 10.2 %all-to-all-start.2 = ((f32[32,1,480]{2,1,0:T(1,128)}), f32[32,1,480]{2,1,0:T(1,128)S(1)}, u32[]{:S(2)}, u32[]{:S(2)}) async-start(f32[32,1,480]{2,1,0:T(1,128)} %reshape.254), calls=%async_computation.3 | async-start | bytes 131072 | tf_op jit(solution)/shard_map/all_to_all | solution.py:33
  256.6 0.2 copy.52
  256.8 0.0 copy-done.1
  256.8 0.8 reshape_reshape.3
  257.6 1.5 reshape.182
  259.1 0.8 copy.50
  259.8 0.9 gather_fusion
  260.7 0.1 gather.23
  260.8 4.5 %all-to-all-done.2 = f32[32,1,480]{2,1,0:T(1,128)S(1)} async-done(((f32[32,1,480]{2,1,0:T(1,128)}), f32[32,1,480]{2,1,0:T(1,128)S(1)}, u32[]{:S(2)}, u32[]{:S(2)}) %all-to-all-start.2) | async-done | bytes 61472 | tf_op jit(solution)/shard_map/all_to_all | solution.py:33
  265.3 0.5 broadcast.167
  265.8 0.8 reduce.15
  266.6 0.1 reshape.255
  266.8 0.1 fusion.19
  267.5 0.5 broadcast.166
  268.0 0.7 fusion.18
  268.6 0.1 add.104
  268.8 0.7 gather_fusion.1
  269.5 0.1 sub.88
  269.6 0.1 copy.55
  269.6 0.1 broadcast_in_dim.68
  269.7 0.1 copy.53
  269.8 1.2 fusion.13
  271.1 0.1 copy.56
  271.2 0.1 broadcast_in_dim.71
  271.2 0.6 broadcast_in_dim.72
  271.9 5.3 %all-to-all-start.5 = ((f32[32,1,32]{2,1,0:T(1,128)}), f32[32,1,32]{2,1,0:T(1,128)S(1)}, u32[]{:S(2)}, u32[]{:S(2)}) async-start(f32[32,1,32]{2,1,0:T(1,128)} %broadcast_in_dim.72), calls=%async_computation.6 | async-start | bytes 32768 | tf_op jit(solution)/shard_map/all_to_all | solution.py:33
  277.2 0.6 fusion.15
  277.7 8.0 %all-to-all-done.5 = f32[32,1,32]{2,1,0:T(1,128)S(1)} async-done(((f32[32,1,32]{2,1,0:T(1,128)}), f32[32,1,32]{2,1,0:T(1,128)S(1)}, u32[]{:S(2)}, u32[]{:S(2)}) %all-to-all-start.5) | async-done | bytes 4128 | tf_op jit(solution)/shard_map/all_to_all | solution.py:33
  285.7 1.8 multiply_divide_fusion
  (45 shorter events, 0.7 us)
Async XLA Ops:
  150.2 2.5 copy-start
  154.4 10.0 %all-to-all-start.1 = ((f32[8,1,1280]{2,1,0:T(1,128)}), f32[8,1,1280]{2,1,0:T(1,128)S(1)}, u32[]{:S(2)}, u32[]{:S(2)}) async-start(f32[8,1,1280]{2,1,0:T(1,128)} %broadcast_in_dim.59), calls=%async_computation.1 | async-start | bytes 81920 | tf_op jit(solution)/shard_map/all_to_all | solution.py:33
  158.9 83.5 %reduce-scatter.2.cloned.1.call-start = ((), (), s32[]{:S(2)}) async-start(), calls=%async_computation.7 | async-start | bytes 11796480 | tf_op jit(solution)/shard_map/reduce_scatter | solution.py:110
  182.3 0.7 copy-start.3
  182.3 61.5 %copy-start.2 = (s32[160]{0:T(256)S(1)}, s32[160]{0:T(256)}, u32[]{:S(2)}) copy-start(s32[160]{0:T(256)} %param.10) | copy-start | bytes 1924
  188.7 15.4 %all-to-all-start.3 = ((f32[8,4,1,2048]{3,1,2,0:T(4,128)}), f32[8,4,1,2048]{3,1,2,0:T(4,128)S(1)}, u32[]{:S(2)}, u32[]{:S(2)}) async-start(f32[8,4,1,2048]{3,1,2,0:T(4,128)} %select_n.68), calls=%async_computation.4 | async-start | bytes 524288 | tf_op jit(solution)/shard_map/all_to_all | solution.py:88
  205.0 41.5 %all-to-all-start.4 = ((f32[8,4,1,2048]{3,0,2,1:T(8,128)}), f32[8,4,1,2048]{3,0,2,1:T(8,128)S(1)}, u32[]{:S(2)}, u32[]{:S(2)}) async-start(f32[8,4,1,2048]{3,0,2,1:T(8,128)} %copy.51), calls=%async_computation.5 | async-start | bytes 524288 | tf_op jit(solution)/shard_map/all_to_all | solution.py:88
  246.5 10.4 %copy-start.1 = (f32[8,4,1,2048]{3,0,2,1:T(8,128)}, f32[8,4,1,2048]{3,0,2,1:T(8,128)S(1)}, u32[]{:S(2)}) copy-start(f32[8,4,1,2048]{3,0,2,1:T(8,128)S(1)} %all-to-all-done.4) | copy-start | bytes 786436
  246.5 18.9 %all-to-all-start.2 = ((f32[32,1,480]{2,1,0:T(1,128)}), f32[32,1,480]{2,1,0:T(1,128)S(1)}, u32[]{:S(2)}, u32[]{:S(2)}) async-start(f32[32,1,480]{2,1,0:T(1,128)} %reshape.254), calls=%async_computation.3 | async-start | bytes 131072 | tf_op jit(solution)/shard_map/all_to_all | solution.py:33
  271.9 13.8 %all-to-all-start.5 = ((f32[32,1,32]{2,1,0:T(1,128)}), f32[32,1,32]{2,1,0:T(1,128)S(1)}, u32[]{:S(2)}, u32[]{:S(2)}) async-start(f32[32,1,32]{2,1,0:T(1,128)} %broadcast_in_dim.72), calls=%async_computation.6 | async-start | bytes 32768 | tf_op jit(solution)/shard_map/all_to_all | solution.py:33
Sparse Core Ops, SparseCore 0:
  182.4 59.8 reduce-scatter.1
